TPU v7x, 32 devices: a whole 2x2x4 slice. The times are simulated.
32 devices in a mesh: dp: 16 (over z, x, core), owner: 2 (over y).
Axes of the slice: x: 2, y: 2, z: 4, core: 2. Of those that a mesh axis runs over, the one named last changes fastest.
Arguments:
- edge_in: bfloat16 [2, 8192, 512], P(None, ('dp', 'owner')), may hold values from -256 to 256
- edge_grad: bfloat16 [2, 8192, 512], P(None, ('dp', 'owner')), may hold values from -1.1953125 to 1.1953125
- row_mask: int32 [2, 8192], P(None, ('dp', 'owner')), may hold values 0 or 1
- layer_at: int32 [2], replicated, may hold values from 0 to 1, each once
Outputs:
- update: bfloat16 [2, 512, 512], P('owner')
Inputs may be any that keep to these rules, and one draw needn't show every extreme that they name: `layer_at`: every layer number appears once.
All inputs are finite; a program needn't handle non-finite values. No bound on the sum of `row_mask` on one device may be relied on, other than what follows from the above.
Results may differ from a plain program's by a relative error of at most 0.0085.
Values may be sent and summed in bfloat16 or wider, within the bound.
A program may use at most 64 MiB of HBM per device.

v0:
```python
import math

import jax
import jax.numpy as jnp
from jax import lax
from jax.sharding import PartitionSpec as P

ITERS = 4


def product(left, right):
    return jnp.einsum("sij,sjk->sik", left, right, precision=lax.Precision.HIGHEST)


def damp_start(factor, width):
    eye = jnp.eye(width, dtype=jnp.float32)
    trace_value = jnp.trace(factor, axis1=1, axis2=2)
    damped = factor + (trace_value * (0.05 / width))[:, None, None] * eye
    size_sq = jnp.sqrt(jnp.sum(damped * damped, axis=(1, 2)) + 1e-06)
    return (damped, eye / size_sq[:, None, None])


def local_terms(inputs, grads, weights, rows_all):
    kept_in = inputs * weights[..., None]
    kept_grad = grads * weights[..., None]
    term_in = (
        jnp.einsum("lrd,lre->lde", kept_in, kept_in, preferred_element_type=jnp.float32)
        * (1.0 / rows_all)
    ).astype(jnp.bfloat16)
    term_out = (
        jnp.einsum("lrd,lre->lde", kept_grad, kept_grad, preferred_element_type=jnp.float32)
        * (1.0 / rows_all)
    ).astype(jnp.bfloat16)
    term_grad = (
        jnp.einsum("lrd,lre->lde", inputs, grads, preferred_element_type=jnp.float32)
        * (1.0 / math.sqrt(rows_all))
    ).astype(jnp.bfloat16)
    return (term_in, term_out, term_grad)


def local(edge_in, edge_grad, row_mask, layer_at):
    rows = edge_in.shape[1]
    width = edge_in.shape[2]
    rows_all = rows * lax.axis_size("dp") * lax.axis_size("owner")
    inputs = jnp.take(edge_in, layer_at, axis=0)
    grads = jnp.take(edge_grad, layer_at, axis=0)
    weights = jnp.take(row_mask, layer_at, axis=0).astype(jnp.bfloat16)
    owned_in, owned_grad, owned_weight = (
        lax.all_to_all(inputs, "owner", split_axis=0, concat_axis=1, tiled=True),
        lax.all_to_all(grads, "owner", split_axis=0, concat_axis=1, tiled=True),
        lax.all_to_all(weights, "owner", split_axis=0, concat_axis=1, tiled=True),
    )
    sources = lax.axis_size("owner")
    slots = owned_in.shape[0]
    owned_in = owned_in.reshape(slots * sources, rows, width)
    owned_grad = owned_grad.reshape(slots * sources, rows, width)
    owned_weight = owned_weight.reshape(slots * sources, rows)
    term_in, term_out, term_grad = local_terms(owned_in, owned_grad, owned_weight, rows_all)
    sum_in = jnp.sum(term_in.astype(jnp.float32).reshape(slots, sources, width, width), axis=1)
    sum_out = jnp.sum(term_out.astype(jnp.float32).reshape(slots, sources, width, width), axis=1)
    sum_grad = jnp.sum(term_grad.astype(jnp.float32).reshape(slots, sources, width, width), axis=1)
    factor_in, factor_out, grad = lax.psum((sum_in, sum_out, sum_grad), "dp")
    damped_in, approx_in = damp_start(factor_in, width)
    damped_out, approx_out = damp_start(factor_out, width)
    for step in range(ITERS):
        approx_in = 2.0 * approx_in - product(approx_in, product(damped_in, approx_in))
        approx_out = 2.0 * approx_out - product(approx_out, product(damped_out, approx_out))
    update = product(product(approx_in, grad), approx_out)
    return update.astype(jnp.bfloat16)


def solution(mesh):
    in_specs = (
        P(None, ("dp", "owner"), None),
        P(None, ("dp", "owner"), None),
        P(None, ("dp", "owner")),
        P(),
    )
    out_specs = P("owner", None, None)
    return jax.shard_map(local, mesh=mesh, in_specs=in_specs, out_specs=out_specs, check_vma=False)
```

profile of v0, /device:TPU:1, one launch (start us, length us, event | category | flops | bytes accessed | tf_op | source)
XLA Modules:
  0.0 194.3 jit_solution(3414564383545405395)
XLA Ops:
  6.5 0.0 copy-start
  6.5 0.7 compare_and_fusion
  7.3 0.7 compare_select_fusion
  8.0 1.2 gather_fusion
  9.2 0.1 fusion.41
  9.3 0.5 broadcast.177
  9.8 0.7 reduce.10
  10.4 0.6 reshape.259
  11.1 3.3 %all-to-all-start.1 = ((bf16[2,2,128]{2,1,0:T(2,128)(2,1)}), bf16[2,2,128]{2,1,0:T(2,128)(2,1)S(1)}, u32[]{:S(2)}, u32[]{:S(2)}) async-start(bf16[2,2,128]{2,1,0:T(2,128)(2,1)} %reshape.259), calls=%async_computation.1 | async-start | bytes 2048 | tf_op jit(solution)/shard_map/all_to_all | solution.py:51
  14.4 0.0 copy-done
  14.4 0.6 gather_fusion.2
  15.0 0.0 copy-done.4
  15.0 0.6 gather_fusion.1
  15.6 1.0 broadcast_select_fusion
  16.5 0.9 all-to-all-done.1
  17.4 8.9 %all_to_all.13 = bf16[2,256,512]{2,1,0:T(8,128)(2,1)S(1)} all-to-all(bf16[2,256,512]{2,1,0:T(8,128)(2,1)S(1)} %get-tuple-element.9), channel_id=1, replica_groups=mesh['dp'=16,'owner'=2] {'owner'}, dimensions={0} | all-to-all | bytes 1048576 | tf_op jit(solution)/shard_map/all_to_all | solution.py:50
  26.3 3.5 %all-to-all-start = ((bf16[2,256,512]{2,1,0:T(8,128)(2,1)}), bf16[2,256,512]{2,1,0:T(8,128)(2,1)S(1)}, u32[]{:S(2)}, u32[]{:S(2)}) async-start(bf16[2,256,512]{2,1,0:T(8,128)(2,1)} %get-tuple-element.10), calls=%async_computation | async-start | bytes 1048576 | tf_op jit(solution)/shard_map/all_to_all | solution.py:49
  29.8 0.0 all-reduce.3.cloned.1.call-start
  29.9 5.3 %all-to-all-done = bf16[2,256,512]{2,1,0:T(8,128)(2,1)S(1)} async-done(((bf16[2,256,512]{2,1,0:T(8,128)(2,1)}), bf16[2,256,512]{2,1,0:T(8,128)(2,1)S(1)}, u32[]{:S(2)}, u32[]{:S(2)}) %all-to-all-start) | async-done | bytes 524320 | tf_op jit(solution)/shard_map/all_to_all | solution.py:49
  35.2 1.5 convert_reduce_fusion.1
  36.7 1.6 convert_reduce_fusion
  38.3 1.6 convert_reduce_fusion.2
  39.9 0.0 all-reduce.3.cloned.1.call-update
  40.0 106.5 %all-reduce.3.cloned.1.call-done = (f32[1,512,512]{2,1,0:T(8,128)}, f32[512,512]{1,0:T(8,128)}, f32[1,512,512]{2,1,0:T(8,128)}) async-done(((f32[1,512,512]{2,1,0:T(8,128)}, f32[512,512]{1,0:T(8,128)}, f32[1,512,512]{2,1,0:T(8,128)}), (f32[1,512,512]{2,1,0:T(8,128)}, f32[512,512]{1,0:T(8,128)}, f32[1,512,512]{2,1,0:T(8,128)})) %all-reduce.3.cloned.1.call-update) | async-done | bytes 3145744 | tf_op jit(solution)/shard_map/psum | solution.py:62
  146.4 2.0 %select_reduce_fusion = f32[]{:T(128)} fusion(f32[1,512,512]{2,1,0:T(8,128)} %get-tuple-element.8), kind=kLoop, calls=%fused_computation.45 | loop fusion | flops 786431 | bytes 1048580 | tf_op jit(solution)/shard_map/jit(trace)/reduce_sum | solution.py:17
  148.5 0.0 copy-done.1
  148.5 0.7 select_reduce_fusion.1
  150.4 0.0 copy-done.2
  150.4 1.0 multiply_reduce_fusion
  152.8 1.8 fusion.2
  154.6 1.8 fusion.11
  156.5 1.9 fusion.19
  158.3 1.8 convolution_subtract_fusion.2
  160.2 1.9 fusion.17
  162.1 2.0 %convolution_subtract_fusion.1 = f32[512,512]{1,0:T(8,128)S(1)} fusion(f32[512,512]{1,0:T(8,128)S(1)} %convolution_subtract_fusion.2, f32[512,512]{1,0:T(8,128)S(1)} %fusion.17), kind=kOutput, calls=%fused_computation.22 | convolution fusion | flops 1611137024 | bytes 3145728 | tf_op jit(solution)/shard_map/sij,sjk->sik/dot_general | solution.py:12
  164.1 1.9 fusion.15
  166.0 1.8 convolution_subtract_fusion
  167.9 1.8 fusion.6
  169.7 1.8 fusion.8
  171.5 1.9 fusion.26
  173.4 1.8 convolution_subtract_fusion.5
  175.2 1.9 fusion.24
  177.1 2.1 %convolution_subtract_fusion.4 = f32[512,512]{1,0:T(8,128)S(1)} fusion(f32[512,512]{1,0:T(8,128)S(1)} %convolution_subtract_fusion.5, f32[512,512]{1,0:T(8,128)S(1)} %fusion.24), kind=kOutput, calls=%fused_computation.25 | convolution fusion | flops 1611137024 | bytes 3145728 | tf_op jit(solution)/shard_map/sij,sjk->sik/dot_general | solution.py:12
  179.2 1.9 fusion.22
  181.1 0.0 copy-start.3
  181.1 1.8 convolution_subtract_fusion.3
  183.0 1.8 fusion.52
  184.8 2.6 %fusion.14 = bf16[1,512,512]{2,1,0:T(8,128)(2,1)} fusion(f32[512,512]{1,0:T(8,128)S(1)} %fusion.52, f32[512,512]{1,0:T(8,128)S(1)} %convolution_subtract_fusion), kind=kOutput, calls=%fused_computation.28 | convolution fusion | flops 1610874880 | bytes 2621440 | tf_op jit(solution)/shard_map/sij,sjk->sik/dot_general | solution.py:12
  (7 shorter events, 0.0 us)
Async XLA Ops:
  6.5 7.8 %copy-start = (bf16[2,256,512]{2,1,0:T(8,128)(2,1)S(1)}, bf16[2,256,512]{2,1,0:T(8,128)(2,1)}, u32[]{:S(2)}) copy-start(bf16[2,256,512]{2,1,0:T(8,128)(2,1)} %param.7) | copy-start | bytes 1572868
  6.5 8.4 %copy-start.4 = (bf16[2,256,512]{2,1,0:T(8,128)(2,1)S(1)}, bf16[2,256,512]{2,1,0:T(8,128)(2,1)}, u32[]{:S(2)}) copy-start(bf16[2,256,512]{2,1,0:T(8,128)(2,1)} %param.6) | copy-start | bytes 1572868
  11.1 6.3 %all-to-all-start.1 = ((bf16[2,2,128]{2,1,0:T(2,128)(2,1)}), bf16[2,2,128]{2,1,0:T(2,128)(2,1)S(1)}, u32[]{:S(2)}, u32[]{:S(2)}) async-start(bf16[2,2,128]{2,1,0:T(2,128)(2,1)} %reshape.259), calls=%async_computation.1 | async-start | bytes 2048 | tf_op jit(solution)/shard_map/all_to_all | solution.py:51
  26.3 8.9 %all-to-all-start = ((bf16[2,256,512]{2,1,0:T(8,128)(2,1)}), bf16[2,256,512]{2,1,0:T(8,128)(2,1)S(1)}, u32[]{:S(2)}, u32[]{:S(2)}) async-start(bf16[2,256,512]{2,1,0:T(8,128)(2,1)} %get-tuple-element.10), calls=%async_computation | async-start | bytes 1048576 | tf_op jit(solution)/shard_map/all_to_all | solution.py:49
  29.8 116.6 %all-reduce.3.cloned.1.call-start = ((), (), s32[]{:S(2)}) async-start(), calls=%async_computation.3 | async-start | bytes 6291456 | tf_op jit(solution)/shard_map/psum | solution.py:62
  146.4 2.1 %copy-start.1 = (f32[1,512,512]{2,1,0:T(8,128)S(1)}, f32[1,512,512]{2,1,0:T(8,128)}, u32[]{:S(2)}) copy-start(f32[1,512,512]{2,1,0:T(8,128)} %get-tuple-element.6) | copy-start | bytes 3145732
  146.4 4.0 %copy-start.2 = (f32[1,512,512]{2,1,0:T(8,128)S(1)}, f32[1,512,512]{2,1,0:T(8,128)}, u32[]{:S(2)}) copy-start(f32[1,512,512]{2,1,0:T(8,128)} %get-tuple-element.8) | copy-start | bytes 3145732
  181.1 1.9 copy-start.3
Sparse Core Ops, SparseCore 0:
  40.1 106.2 all-reduce.2
where the time goes:
time: 197 us; the launch traced here: 194 us
  waiting for transfers between devices  113 us (57%)
  matrix products  39.2 us (20%)
  between operations  16.3 us (8%)
  blocking collectives  8.89 us (5%)
  starting transfers between devices  6.86 us (3%)
  other arithmetic  6.8 us (3%)
  local copies, waits for them, and re-layouts  3.57 us (2%)
    psum x1, waiting for transfers between devices, local(): factor_in, factor_out, grad = lax.psum((sum_in, sum_out, sum_grad), 'dp')  106 us
    dot_general x18, matrix products, product(): jnp.einsum('sij,sjk->sik', left, right, precision=lax.Precision.HIGHEST)  34.5 us
    all_to_all x1, blocking collectives, local(): lax.all_to_all(grads, 'owner', split_axis=0, concat_axis=1, tiled=True)  8.89 us
    all_to_all x1, waiting for transfers between devices, local(): lax.all_to_all(inputs, 'owner', split_axis=0, concat_axis=1, tiled=True)  5.34 us
  transfers between devices with their start and end apart: 3, of which 3 were waited for; matrix products, arithmetic and copies ran while one was open for 1% of the time, Pallas kernels for 0%

commit v1 on v0

v1 whole, which is shorter than its diff:
```python
import functools
import math

import jax
import jax.numpy as jnp
from jax import lax
from jax.experimental import pallas as pl
from jax.experimental.pallas import tpu as pltpu
from jax.sharding import PartitionSpec as P

MESH = pl.DeviceIdType.MESH
F32 = jnp.float32
BF16 = jnp.bfloat16


def mm(left, right):
    return jnp.dot(left, right, preferred_element_type=F32)


def mm_rows(left, right):
    return lax.dot_general(left, right, (((0,), (0,)), ((), ())), preferred_element_type=F32)


def kernel(
    owners, chips, slots, rows, width, rows_all,
    edge_in, edge_grad, mask, layer_at, out,
    picked, picked_mask, rows_got, mask_got,
    give, got, split, split_got, total, halves, inverse,
    row_send, row_recv, mask_send, mask_recv, core_send, core_recv,
    split_send, split_recv, total_send, total_recv,
):
    dp = lax.axis_index("dp")
    me = lax.axis_index("owner")
    chip = dp // 2
    core = lax.rem(dp, 2)
    other = 1 - core
    half = width // 2
    part = (width + half) // chips

    barrier = pltpu.get_barrier_semaphore()

    def owner_at(k):
        return {"dp": dp, "owner": lax.rem(me + k, owners)}

    def chip_at(k):
        return {"dp": lax.rem(chip + k, chips) * 2 + core, "owner": me}

    partner = {"dp": chip * 2 + other, "owner": me}
    peers = [owner_at(k) for k in range(1, owners)]
    peers += [chip_at(k) for k in range(1, chips)]
    peers += [partner]
    for peer in peers:
        pl.semaphore_signal(barrier, inc=1, device_id=peer, device_id_type=MESH)

    for q in range(owners):
        for s in range(slots):
            layer = layer_at[q * slots + s]
            picked[q, 0, s] = edge_in[layer]
            picked[q, 1, s] = edge_grad[layer]
            line = mask[pl.ds(layer, 1), :].astype(F32)
            picked_mask[q, s] = jnp.broadcast_to(line, (8, rows))
    pl.semaphore_wait(barrier, len(peers))

    def copy(src, dst, send, recv, device):
        made = pltpu.make_async_remote_copy(
            src_ref=src, dst_ref=dst, send_sem=send, recv_sem=recv,
            device_id=device, device_id_type=MESH,
        )
        made.start()
        return made

    started = []
    row_copies = []
    for k in range(1, owners):
        to = lax.rem(me + k, owners)
        row_copies.append(copy(picked_mask.at[to], mask_got.at[k - 1], mask_send.at[k - 1], mask_recv.at[k - 1], owner_at(k)))
    for t in range(2):
        for k in range(1, owners):
            to = lax.rem(me + k, owners)
            row_copies.append(copy(picked.at[to, t], rows_got.at[k - 1, t], row_send.at[k - 1, t], row_recv.at[k - 1, t], owner_at(k)))
    for c in row_copies:
        c.wait_recv()
    started += row_copies

    def kept(values, line):
        column = jnp.broadcast_to(line[0:1, :], (128, rows)).T
        column = jnp.concatenate([column] * (width // 128), axis=1)
        return (values.astype(F32) * column).astype(BF16)

    def terms(c, s):
        factor = None
        cross = None
        for k in range(owners):
            if k == 0:
                block, line = picked.at[me], picked_mask[me, s]
            else:
                block, line = rows_got.at[k - 1], mask_got[k - 1, s]
            values = kept(block[c, s], line)
            left = block[0, s, :, pl.ds(pl.multiple_of(c * half, half), half)]
            a = mm_rows(values, values)
            b = mm_rows(left, block[1, s])
            factor = a if factor is None else factor + a
            cross = b if cross is None else cross + b
        return factor * (1.0 / rows_all), cross * (1.0 / math.sqrt(rows_all))

    core_copies = []
    for s in range(slots):
        factor, cross = terms(other, s)
        give[s, :width] = factor.astype(BF16)
        give[s, width:] = cross.astype(BF16)
        core_copies.append(copy(give.at[s], got.at[s], core_send.at[s], core_recv.at[s], partner))
    started += core_copies

    for s in range(slots):
        factor, cross = terms(core, s)
        core_copies[s].wait_recv()
        both = jnp.concatenate([factor, cross], axis=0) + got[s].astype(F32)
        split[:, s] = both.astype(BF16).reshape(chips, part, width)

    split_copies = []
    for k in range(1, chips):
        to = lax.rem(chip + k, chips)
        split_copies.append(copy(split.at[to], split_got.at[k - 1], split_send.at[k - 1], split_recv.at[k - 1], chip_at(k)))
    started += split_copies
    summed = split[chip].astype(F32)
    for k in range(1, chips):
        split_copies[k - 1].wait_recv()
        summed += split_got[k - 1].astype(F32)
    total[chip] = summed.astype(BF16)

    total_copies = []
    for k in range(1, chips):
        total_copies.append(copy(total.at[chip], total.at[chip], total_send.at[k - 1], total_recv.at[k - 1], chip_at(k)))
    started += total_copies
    for c in total_copies:
        c.wait_recv()

    at_row = lax.broadcasted_iota(jnp.int32, (width, width), 0)
    at_column = lax.broadcasted_iota(jnp.int32, (width, width), 1)
    eye = (at_row == at_column).astype(F32)
    half_copies = []
    inverse_copies = []
    for s in range(slots):
        whole = total[:, s].reshape(width + half, width)
        halves[core, s] = whole[width:]
        half_copies.append(copy(halves.at[core, s], halves.at[core, s], core_send.at[slots + s], core_recv.at[slots + s], partner))
    for s in range(slots):
        whole = total[:, s].reshape(width + half, width)
        factor = whole[:width].astype(F32)
        damped = factor + (jnp.sum(factor * eye) * (0.05 / width)) * eye
        scale = lax.rsqrt(jnp.sum(damped * damped) + 1e-06)
        near = damped * scale
        approx = 2.0 * eye - near
        near_low = near.astype(BF16)
        near = 2.0 * near - mm(near_low, near_low)
        for step in range(3):
            near_low = near.astype(BF16)
            approx = 2.0 * approx - mm(approx.astype(BF16), near_low)
            if step < 2:
                near = 2.0 * near - mm(near_low, near_low)
        inverse[core, s] = (approx * scale).astype(BF16)
        inverse_copies.append(copy(inverse.at[core, s], inverse.at[core, s], core_send.at[2 * slots + s], core_recv.at[2 * slots + s], partner))
    started += half_copies + inverse_copies
    for s in range(slots):
        half_copies[s].wait_recv()
        inverse_copies[s].wait_recv()
        grad = halves[:, s].reshape(width, width)
        left = mm(inverse[0, s], grad)
        out[s] = mm(left.astype(BF16), inverse[1, s]).astype(BF16)
    for c in started:
        c.wait_send()


def solution(mesh):
    owners = mesh.shape["owner"]
    chips = mesh.shape["dp"] // 2

    def local(edge_in, edge_grad, row_mask, layer_at):
        layers, rows, width = edge_in.shape
        slots = layers // owners
        rows_all = rows * mesh.shape["dp"] * owners
        high = width + width // 2
        part = high // chips
        others = max(owners - 1, 1)
        vmem = pl.BlockSpec(memory_space=pltpu.VMEM)
        dma = pltpu.SemaphoreType.DMA
        return pl.pallas_call(
            functools.partial(kernel, owners, chips, slots, rows, width, rows_all),
            out_shape=jax.ShapeDtypeStruct((slots, width, width), BF16),
            in_specs=[vmem, vmem, vmem, pl.BlockSpec(memory_space=pltpu.SMEM)],
            out_specs=vmem,
            scratch_shapes=[
                pltpu.VMEM((owners, 2, slots, rows, width), BF16),
                pltpu.VMEM((owners, slots, 8, rows), F32),
                pltpu.VMEM((others, 2, slots, rows, width), BF16),
                pltpu.VMEM((others, slots, 8, rows), F32),
                pltpu.VMEM((slots, high, width), BF16),
                pltpu.VMEM((slots, high, width), BF16),
                pltpu.VMEM((chips, slots, part, width), BF16),
                pltpu.VMEM((chips - 1, slots, part, width), BF16),
                pltpu.VMEM((chips, slots, part, width), BF16),
                pltpu.VMEM((2, slots, width // 2, width), BF16),
                pltpu.VMEM((2, slots, width, width), BF16),
                dma((others, 2)), dma((others, 2)),
                dma((others,)), dma((others,)),
                dma((3 * slots,)), dma((3 * slots,)),
                dma((chips - 1,)), dma((chips - 1,)),
                dma((chips - 1,)), dma((chips - 1,)),
            ],
            compiler_params=pltpu.CompilerParams(
                collective_id=0, has_side_effects=True, vmem_limit_bytes=60 * 1024 * 1024,
            ),
        )(edge_in, edge_grad, row_mask, layer_at)

    in_specs = (
        P(None, ("dp", "owner"), None),
        P(None, ("dp", "owner"), None),
        P(None, ("dp", "owner")),
        P(),
    )
    return jax.shard_map(local, mesh=mesh, in_specs=in_specs, out_specs=P("owner", None, None), check_vma=False)
```

time: 197 us -> 67 us (0.34)
  the two profiles are of different devices: /device:TPU:1 before, /device:TPU:27 now
where the time goes in v1:
time: 67 us; the launch traced here: 66.9 us
  Pallas kernels  65 us (97%)
  local copies, waits for them, and re-layouts  1.87 us (3%)
    pallas_call x1, Pallas kernels, local(): pl.pallas_call(functools.partial(kernel, owners, chips, slots, rows, widt...  65 us
    unnamed x1, local copies, waits for them, and re-layouts  1.87 us

profile of v1, /device:TPU:27, one launch (start us, length us, event | category | flops | bytes accessed | tf_op | source)
XLA Modules:
  0.0 66.9 jit_solution(17313216011732528855)
XLA Ops:
  0.0 65.0 %shard_map.46 = bf16[1,512,512]{2,1,0:T(8,128)(2,1)} custom-call(bf16[2,256,512]{2,1,0:T(8,128)(2,1)} %edge_in.1, bf16[2,256,512]{2,1,0:T(8,128)(2,1)} %edge_grad.1, s32[2,256]{1,0:T(2,128)} %mask.1, s32[2]{0:T(128)} %layer_at.1), custom_call_target="tpu_custom_call" | custom-call | tf_op jit(solution)/shard_map/pallas_call | solution.py:187
  65.0 1.9 %copy.6 = bf16[1,512,512]{2,1,0:T(8,128)(2,1)} copy(bf16[1,512,512]{2,1,0:T(8,128)(2,1)} %shard_map.46) | data formatting | bytes 1048576

commit v2 on v1

--- a/solution.py
+++ b/solution.py
@@ -11,6 +11,7 @@
 MESH = pl.DeviceIdType.MESH
 F32 = jnp.float32
 BF16 = jnp.bfloat16
+TILE = 128
 
 
 def mm(left, right):
@@ -25,9 +26,10 @@
     owners, chips, slots, rows, width, rows_all,
     edge_in, edge_grad, mask, layer_at, out,
     picked, picked_mask, rows_got, mask_got,
-    give, got, split, split_got, total, halves, inverse,
+    give, got, split, pair_got, passing, line_got, total, full, halves, inverse,
     row_send, row_recv, mask_send, mask_recv, core_send, core_recv,
-    split_send, split_recv, total_send, total_recv,
+    pair_send, pair_recv, line_send, line_recv,
+    spread_send, spread_recv, across_send, across_recv,
 ):
     dp = lax.axis_index("dp")
     me = lax.axis_index("owner")
@@ -35,20 +37,26 @@
     core = lax.rem(dp, 2)
     other = 1 - core
     half = width // 2
-    part = (width + half) // chips
+    part = TILE // chips
+    tiles = width // TILE
+    lines = chips // 2
+    line = chip // 2
+    side = lax.rem(chip, 2)
 
     barrier = pltpu.get_barrier_semaphore()
 
     def owner_at(k):
         return {"dp": dp, "owner": lax.rem(me + k, owners)}
 
-    def chip_at(k):
-        return {"dp": lax.rem(chip + k, chips) * 2 + core, "owner": me}
+    def line_at(k):
+        return {"dp": (lax.rem(line + k, lines) * 2 + side) * 2 + core, "owner": me}
+
+    pair = {"dp": (line * 2 + 1 - side) * 2 + core, "owner": me}
 
     partner = {"dp": chip * 2 + other, "owner": me}
     peers = [owner_at(k) for k in range(1, owners)]
-    peers += [chip_at(k) for k in range(1, chips)]
-    peers += [partner]
+    peers += [line_at(k) for k in range(1, lines)]
+    peers += [pair, partner]
     for peer in peers:
         pl.semaphore_signal(barrier, inc=1, device_id=peer, device_id_type=MESH)
 
@@ -57,8 +65,8 @@
             layer = layer_at[q * slots + s]
             picked[q, 0, s] = edge_in[layer]
             picked[q, 1, s] = edge_grad[layer]
-            line = mask[pl.ds(layer, 1), :].astype(F32)
-            picked_mask[q, s] = jnp.broadcast_to(line, (8, rows))
+            mask_row = mask[pl.ds(layer, 1), :].astype(F32)
+            picked_mask[q, s] = jnp.broadcast_to(mask_row, (8, rows))
     pl.semaphore_wait(barrier, len(peers))
 
     def copy(src, dst, send, recv, device):
@@ -88,52 +96,79 @@
         return (values.astype(F32) * column).astype(BF16)
 
     def terms(c, s):
-        factor = None
-        cross = None
+        sums = {}
         for k in range(owners):
             if k == 0:
-                block, line = picked.at[me], picked_mask[me, s]
+                block, line_mask = picked.at[me], picked_mask[me, s]
             else:
-                block, line = rows_got.at[k - 1], mask_got[k - 1, s]
-            values = kept(block[c, s], line)
+                block, line_mask = rows_got.at[k - 1], mask_got[k - 1, s]
+            values = kept(block[c, s], line_mask)
             left = block[0, s, :, pl.ds(pl.multiple_of(c * half, half), half)]
-            a = mm_rows(values, values)
-            b = mm_rows(left, block[1, s])
-            factor = a if factor is None else factor + a
-            cross = b if cross is None else cross + b
-        return factor * (1.0 / rows_all), cross * (1.0 / math.sqrt(rows_all))
+            made = [mm_rows(values[:, TILE * i:TILE * (i + 1)], values[:, TILE * i:]) for i in range(tiles)]
+            made.append(mm_rows(left, block[1, s]))
+            for i, value in enumerate(made):
+                sums[i] = sums[i] + value if k else value
+        return sums
+
+    def pack(ref, s, sums):
+        at = 0
+        for i in range(tiles):
+            strip = sums[i] * (1.0 / rows_all)
+            for j in range(tiles - i):
+                tile = strip[:, TILE * j:TILE * (j + 1)].reshape(chips, part, TILE)
+                ref[s, :, at] = tile.astype(BF16)
+                at += 1
+        cross = sums[tiles] * (1.0 / math.sqrt(rows_all))
+        for i in range(tiles // 2):
+            for j in range(tiles):
+                tile = cross[TILE * i:TILE * (i + 1), TILE * j:TILE * (j + 1)].reshape(chips, part, TILE)
+                ref[s, :, at] = tile.astype(BF16)
+                at += 1
+
+    def tile_of(s, at):
+        return total[:, s, at].astype(F32).reshape(TILE, TILE)
 
     core_copies = []
     for s in range(slots):
-        factor, cross = terms(other, s)
-        give[s, :width] = factor.astype(BF16)
-        give[s, width:] = cross.astype(BF16)
+        pack(give, s, terms(other, s))
         core_copies.append(copy(give.at[s], got.at[s], core_send.at[s], core_recv.at[s], partner))
     started += core_copies
 
     for s in range(slots):
-        factor, cross = terms(core, s)
+        pack(split, s, terms(core, s))
         core_copies[s].wait_recv()
-        both = jnp.concatenate([factor, cross], axis=0) + got[s].astype(F32)
-        split[:, s] = both.astype(BF16).reshape(chips, part, width)
-
-    split_copies = []
-    for k in range(1, chips):
-        to = lax.rem(chip + k, chips)
-        split_copies.append(copy(split.at[to], split_got.at[k - 1], split_send.at[k - 1], split_recv.at[k - 1], chip_at(k)))
-    started += split_copies
-    summed = split[chip].astype(F32)
-    for k in range(1, chips):
-        split_copies[k - 1].wait_recv()
-        summed += split_got[k - 1].astype(F32)
+        split[s] = (split[s].astype(F32) + got[s].astype(F32)).astype(BF16)
+
+    order = list(range(1, lines)) + [0]
+    pair_copies = {}
+    for k in order:
+        far = lax.rem(line + k, lines) * 2 + 1 - side
+        pair_copies[k] = copy(split.at[:, far], pair_got.at[k], pair_send.at[k], pair_recv.at[k], pair)
+    line_copies = {}
+    for k in order:
+        near = lax.rem(line + k, lines) * 2 + side
+        pair_copies[k].wait_recv()
+        summed = split[:, near].astype(F32) + pair_got[k].astype(F32)
+        if k:
+            passing[k - 1] = summed.astype(BF16)
+            line_copies[k] = copy(passing.at[k - 1], line_got.at[k - 1], line_send.at[k - 1], line_recv.at[k - 1], line_at(k))
+    for k in range(1, lines):
+        line_copies[k].wait_recv()
+        summed += line_got[k - 1].astype(F32)
     total[chip] = summed.astype(BF16)
-
-    total_copies = []
-    for k in range(1, chips):
-        total_copies.append(copy(total.at[chip], total.at[chip], total_send.at[k - 1], total_recv.at[k - 1], chip_at(k)))
-    started += total_copies
-    for c in total_copies:
+    started += list(pair_copies.values()) + list(line_copies.values())
+
+    spread = {}
+    for k in range(1, lines):
+        spread[k] = copy(total.at[chip], total.at[chip], spread_send.at[k - 1], spread_recv.at[k - 1], line_at(k))
+    across = [copy(total.at[chip], total.at[chip], across_send.at[0], across_recv.at[0], pair)]
+    for k in range(1, lines):
+        spread[k].wait_recv()
+        origin = lax.rem(line - k + lines, lines) * 2 + side
+        across.append(copy(total.at[origin], total.at[origin], across_send.at[k], across_recv.at[k], pair))
+    for c in across:
         c.wait_recv()
+    started += list(spread.values()) + across
 
     at_row = lax.broadcasted_iota(jnp.int32, (width, width), 0)
     at_column = lax.broadcasted_iota(jnp.int32, (width, width), 1)
@@ -141,12 +176,22 @@
     half_copies = []
     inverse_copies = []
     for s in range(slots):
-        whole = total[:, s].reshape(width + half, width)
-        halves[core, s] = whole[width:]
+        at = tiles * (tiles + 1) // 2
+        for i in range(tiles // 2):
+            for j in range(tiles):
+                halves[core, s, TILE * i:TILE * (i + 1), TILE * j:TILE * (j + 1)] = tile_of(s, at).astype(BF16)
+                at += 1
         half_copies.append(copy(halves.at[core, s], halves.at[core, s], core_send.at[slots + s], core_recv.at[slots + s], partner))
     for s in range(slots):
-        whole = total[:, s].reshape(width + half, width)
-        factor = whole[:width].astype(F32)
+        at = 0
+        for i in range(tiles):
+            for j in range(i, tiles):
+                tile = tile_of(s, at)
+                full[TILE * i:TILE * (i + 1), TILE * j:TILE * (j + 1)] = tile
+                if j > i:
+                    full[TILE * j:TILE * (j + 1), TILE * i:TILE * (i + 1)] = tile.T
+                at += 1
+        factor = full[...]
         damped = factor + (jnp.sum(factor * eye) * (0.05 / width)) * eye
         scale = lax.rsqrt(jnp.sum(damped * damped) + 1e-06)
         near = damped * scale
@@ -179,8 +224,10 @@
         layers, rows, width = edge_in.shape
         slots = layers // owners
         rows_all = rows * mesh.shape["dp"] * owners
-        high = width + width // 2
-        part = high // chips
+        tiles = width // TILE
+        count = tiles * (tiles + 1) // 2 + tiles * tiles // 2
+        part = TILE // chips
+        lines = chips // 2
         others = max(owners - 1, 1)
         vmem = pl.BlockSpec(memory_space=pltpu.VMEM)
         dma = pltpu.SemaphoreType.DMA
@@ -194,18 +241,23 @@
                 pltpu.VMEM((owners, slots, 8, rows), F32),
                 pltpu.VMEM((others, 2, slots, rows, width), BF16),
                 pltpu.VMEM((others, slots, 8, rows), F32),
-                pltpu.VMEM((slots, high, width), BF16),
-                pltpu.VMEM((slots, high, width), BF16),
-                pltpu.VMEM((chips, slots, part, width), BF16),
-                pltpu.VMEM((chips - 1, slots, part, width), BF16),
-                pltpu.VMEM((chips, slots, part, width), BF16),
+                pltpu.VMEM((slots, chips, count, part, TILE), BF16),
+                pltpu.VMEM((slots, chips, count, part, TILE), BF16),
+                pltpu.VMEM((slots, chips, count, part, TILE), BF16),
+                pltpu.VMEM((lines, slots, count, part, TILE), BF16),
+                pltpu.VMEM((lines - 1, slots, count, part, TILE), BF16),
+                pltpu.VMEM((lines - 1, slots, count, part, TILE), BF16),
+                pltpu.VMEM((chips, slots, count, part, TILE), BF16),
+                pltpu.VMEM((width, width), F32),
                 pltpu.VMEM((2, slots, width // 2, width), BF16),
                 pltpu.VMEM((2, slots, width, width), BF16),
                 dma((others, 2)), dma((others, 2)),
                 dma((others,)), dma((others,)),
                 dma((3 * slots,)), dma((3 * slots,)),
-                dma((chips - 1,)), dma((chips - 1,)),
-                dma((chips - 1,)), dma((chips - 1,)),
+                dma((lines,)), dma((lines,)),
+                dma((lines - 1,)), dma((lines - 1,)),
+                dma((lines - 1,)), dma((lines - 1,)),
+                dma((lines,)), dma((lines,)),
             ],
             compiler_params=pltpu.CompilerParams(
                 collective_id=0, has_side_effects=True, vmem_limit_bytes=60 * 1024 * 1024,

time: 67 us -> 52.5 us (0.78)
  the two profiles are of different devices: /device:TPU:27 before, /device:TPU:1 now
where the time goes in v2:
time: 52.5 us; the launch traced here: 52.1 us
  Pallas kernels  50.2 us (96%)
  local copies, waits for them, and re-layouts  1.87 us (4%)
    pallas_call x1, Pallas kernels, local(): pl.pallas_call(functools.partial(kernel, owners, chips, slots, rows, widt...  50.2 us
    unnamed x1, local copies, waits for them, and re-layouts  1.87 us

profile of v2, /device:TPU:1, one launch (start us, length us, event | category | flops | bytes accessed | tf_op | source)
XLA Modules:
  0.0 52.1 jit_solution(12781925976153033483)
XLA Ops:
  0.0 50.2 %shard_map.46 = bf16[1,512,512]{2,1,0:T(8,128)(2,1)} custom-call(bf16[2,256,512]{2,1,0:T(8,128)(2,1)} %edge_in.1, bf16[2,256,512]{2,1,0:T(8,128)(2,1)} %edge_grad.1, s32[2,256]{1,0:T(2,128)} %mask.1, s32[2]{0:T(128)} %layer_at.1), custom_call_target="tpu_custom_call" | custom-call | tf_op jit(solution)/shard_map/pallas_call | solution.py:234
  50.2 1.9 %copy.6 = bf16[1,512,512]{2,1,0:T(8,128)(2,1)} copy(bf16[1,512,512]{2,1,0:T(8,128)(2,1)} %shard_map.46) | data formatting | bytes 1048576

commit v3 on v2

v3 whole, which is shorter than its diff:
```python
import functools
import math

import jax
import jax.numpy as jnp
from jax import lax
from jax.experimental import pallas as pl
from jax.experimental.pallas import tpu as pltpu
from jax.sharding import PartitionSpec as P

MESH = pl.DeviceIdType.MESH
F32 = jnp.float32
BF16 = jnp.bfloat16
TILE = 128


def mm(left, right):
    return jnp.dot(left, right, preferred_element_type=F32)


def mm_rows(left, right):
    return lax.dot_general(left, right, (((0,), (0,)), ((), ())), preferred_element_type=F32)


def kernel(
    owners, chips, slots, rows, width, rows_all,
    edge_in, edge_grad, mask, layer_at, out,
    give, got, split, pair_got, crossing, owner_got, passing, line_got, total, full, halves, inverse,
    core_send, core_recv, pair_send, pair_recv, owner_send, owner_recv,
    line_send, line_recv, last_send, last_recv,
    spread_send, spread_recv, across_send, across_recv,
):
    dp = lax.axis_index("dp")
    me = lax.axis_index("owner")
    chip = dp // 2
    core = lax.rem(dp, 2)
    other = 1 - core
    half = width // 2
    part = TILE // chips
    tiles = width // TILE
    lines = chips // 2
    line = chip // 2
    side = lax.rem(chip, 2)

    barrier = pltpu.get_barrier_semaphore()

    def owner_at(k):
        return {"dp": dp, "owner": lax.rem(me + k, owners)}

    def line_at(k):
        return {"dp": (lax.rem(line + k, lines) * 2 + side) * 2 + core, "owner": me}

    pair = {"dp": (line * 2 + 1 - side) * 2 + core, "owner": me}

    partner = {"dp": chip * 2 + other, "owner": me}
    peers = [owner_at(k) for k in range(1, owners)]
    peers += [line_at(k) for k in range(1, lines)]
    peers += [pair, partner]
    for peer in peers:
        pl.semaphore_signal(barrier, inc=1, device_id=peer, device_id_type=MESH)

    def copy(src, dst, send, recv, device):
        made = pltpu.make_async_remote_copy(
            src_ref=src, dst_ref=dst, send_sem=send, recv_sem=recv,
            device_id=device, device_id_type=MESH,
        )
        made.start()
        return made

    started = []

    def terms(c, q, s):
        layer = layer_at[q * slots + s]
        inputs, grads = edge_in[layer], edge_grad[layer]
        column = jnp.broadcast_to(mask[pl.ds(layer, 1), :].astype(F32), (TILE, rows)).T
        column = jnp.concatenate([column] * tiles, axis=1)
        first = c == 0
        values = (jnp.where(first, inputs, grads).astype(F32) * column).astype(BF16)
        left = jnp.where(first, inputs[:, :half], inputs[:, half:])
        made = [mm_rows(values[:, TILE * i:TILE * (i + 1)], values[:, TILE * i:]) for i in range(tiles)]
        made.append(mm_rows(left, grads))
        return made

    def pack(ref, sums):
        at = 0
        for i in range(tiles):
            strip = sums[i] * (1.0 / rows_all)
            for j in range(tiles - i):
                tile = strip[:, TILE * j:TILE * (j + 1)].reshape(chips, part, TILE)
                ref[:, at] = tile.astype(BF16)
                at += 1
        cross = sums[tiles] * (1.0 / math.sqrt(rows_all))
        for i in range(tiles // 2):
            for j in range(tiles):
                tile = cross[TILE * i:TILE * (i + 1), TILE * j:TILE * (j + 1)].reshape(chips, part, TILE)
                ref[:, at] = tile.astype(BF16)
                at += 1

    def tile_of(s, at):
        return total[:, s, at].astype(F32).reshape(TILE, TILE)

    order = list(range(1, lines)) + [0]
    pair_copies = {}
    for o in list(range(1, owners)) + [0]:
        q = lax.rem(me + o, owners)
        core_copies = []
        for s in range(slots):
            pack(give.at[o, s], terms(other, q, s))
            if not started and not core_copies:
                pl.semaphore_wait(barrier, len(peers))
            core_copies.append(copy(give.at[o, s], got.at[o, s], core_send.at[o, s], core_recv.at[o, s], partner))
        for s in range(slots):
            pack(split.at[o, s], terms(core, q, s))
            core_copies[s].wait_recv()
            split[o, s] = (split[o, s].astype(F32) + got[o, s].astype(F32)).astype(BF16)
        started += core_copies
        for k in order:
            far = lax.rem(line + k, lines) * 2 + 1 - side
            pair_copies[o, k] = copy(split.at[o, :, far], pair_got.at[o, k], pair_send.at[o, k], pair_recv.at[o, k], pair)

    owner_copies = {}
    for o in range(1, owners):
        for k in order:
            near = lax.rem(line + k, lines) * 2 + side
            pair_copies[o, k].wait_recv()
            crossing[o - 1, k] = (split[o, :, near].astype(F32) + pair_got[o, k].astype(F32)).astype(BF16)
            owner_copies[o, k] = copy(crossing.at[o - 1, k], owner_got.at[o - 1, k], owner_send.at[o - 1, k], owner_recv.at[o - 1, k], owner_at(o))
    line_copies = {}
    for k in order:
        near = lax.rem(line + k, lines) * 2 + side
        pair_copies[0, k].wait_recv()
        summed = split[0, :, near].astype(F32) + pair_got[0, k].astype(F32)
        for o in range(1, owners):
            owner_copies[o, k].wait_recv()
            summed += owner_got[o - 1, k].astype(F32)
        if k:
            passing[k - 1] = summed.astype(BF16)
            line_copies[k] = copy(passing.at[k - 1], line_got.at[k - 1], line_send.at[k - 1], line_recv.at[k - 1], line_at(k))
    for k in range(1, lines):
        line_copies[k].wait_recv()
        summed += line_got[k - 1].astype(F32)
    total[chip] = summed.astype(BF16)
    for group in (pair_copies, owner_copies, line_copies):
        started += list(group.values())

    pairs = tiles * (tiles + 1) // 2
    across, spread = [], []
    for g, (low, high) in enumerate(((0, pairs), (pairs, pairs + tiles * tiles // 2))):
        across.append([])
        spread_g = []
        for k in range(1, lines):
            piece = total.at[chip, :, low:high]
            spread_g.append(copy(piece, piece, spread_send.at[g, k - 1], spread_recv.at[g, k - 1], line_at(k)))
        piece = total.at[chip, :, low:high]
        across[g].append(copy(piece, piece, across_send.at[g, 0], across_recv.at[g, 0], pair))
        started += spread_g
        spread.append(spread_g)
    for g, (low, high) in enumerate(((0, pairs), (pairs, pairs + tiles * tiles // 2))):
        for k in range(1, lines):
            spread[g][k - 1].wait_recv()
            origin = lax.rem(line - k + lines, lines) * 2 + side
            piece = total.at[origin, :, low:high]
            across[g].append(copy(piece, piece, across_send.at[g, k], across_recv.at[g, k], pair))
        started += across[g]
    for c in across[0]:
        c.wait_recv()

    at_row = lax.broadcasted_iota(jnp.int32, (width, width), 0)
    at_column = lax.broadcasted_iota(jnp.int32, (width, width), 1)
    eye = (at_row == at_column).astype(F32)
    inverse_copies = []
    for s in range(slots):
        at = 0
        for i in range(tiles):
            for j in range(i, tiles):
                tile = tile_of(s, at)
                full[TILE * i:TILE * (i + 1), TILE * j:TILE * (j + 1)] = tile
                if j > i:
                    full[TILE * j:TILE * (j + 1), TILE * i:TILE * (i + 1)] = tile.T
                at += 1
        factor = full[...]
        damped = factor + (jnp.sum(factor * eye) * (0.05 / width)) * eye
        scale = lax.rsqrt(jnp.sum(damped * damped) + 1e-06)
        near = damped * scale
        approx = 2.0 * eye - near
        near_low = near.astype(BF16)
        near = 2.0 * near - mm(near_low, near_low)
        for step in range(3):
            near_low = near.astype(BF16)
            approx = 2.0 * approx - mm(approx.astype(BF16), near_low)
            if step < 2:
                near = 2.0 * near - mm(near_low, near_low)
        inverse[core, s] = (approx * scale).astype(BF16)
        inverse_copies.append(copy(inverse.at[core, s], inverse.at[core, s], last_send.at[1, s], last_recv.at[1, s], partner))
    for c in across[1]:
        c.wait_recv()
    half_copies = []
    for s in range(slots):
        at = tiles * (tiles + 1) // 2
        for i in range(tiles // 2):
            for j in range(tiles):
                halves[core, s, TILE * i:TILE * (i + 1), TILE * j:TILE * (j + 1)] = tile_of(s, at).astype(BF16)
                at += 1
        half_copies.append(copy(halves.at[core, s], halves.at[core, s], last_send.at[0, s], last_recv.at[0, s], partner))
    started += half_copies + inverse_copies
    for s in range(slots):
        half_copies[s].wait_recv()
        inverse_copies[s].wait_recv()
        grad = halves[:, s].reshape(width, width)
        left = mm(inverse[0, s], grad)
        out[s] = mm(left.astype(BF16), inverse[1, s]).astype(BF16)
    for c in started:
        c.wait_send()


def solution(mesh):
    owners = mesh.shape["owner"]
    chips = mesh.shape["dp"] // 2

    def local(edge_in, edge_grad, row_mask, layer_at):
        layers, rows, width = edge_in.shape
        slots = layers // owners
        rows_all = rows * mesh.shape["dp"] * owners
        tiles = width // TILE
        count = tiles * (tiles + 1) // 2 + tiles * tiles // 2
        part = TILE // chips
        lines = chips // 2
        others = max(owners - 1, 1)
        vmem = pl.BlockSpec(memory_space=pltpu.VMEM)
        dma = pltpu.SemaphoreType.DMA
        return pl.pallas_call(
            functools.partial(kernel, owners, chips, slots, rows, width, rows_all),
            out_shape=jax.ShapeDtypeStruct((slots, width, width), BF16),
            in_specs=[vmem, vmem, vmem, pl.BlockSpec(memory_space=pltpu.SMEM)],
            out_specs=vmem,
            scratch_shapes=[
                pltpu.VMEM((owners, slots, chips, count, part, TILE), BF16),
                pltpu.VMEM((owners, slots, chips, count, part, TILE), BF16),
                pltpu.VMEM((owners, slots, chips, count, part, TILE), BF16),
                pltpu.VMEM((owners, lines, slots, count, part, TILE), BF16),
                pltpu.VMEM((others, lines, slots, count, part, TILE), BF16),
                pltpu.VMEM((others, lines, slots, count, part, TILE), BF16),
                pltpu.VMEM((lines - 1, slots, count, part, TILE), BF16),
                pltpu.VMEM((lines - 1, slots, count, part, TILE), BF16),
                pltpu.VMEM((chips, slots, count, part, TILE), BF16),
                pltpu.VMEM((width, width), F32),
                pltpu.VMEM((2, slots, width // 2, width), BF16),
                pltpu.VMEM((2, slots, width, width), BF16),
                dma((owners, slots)), dma((owners, slots)),
                dma((owners, lines)), dma((owners, lines)),
                dma((others, lines)), dma((others, lines)),
                dma((lines - 1,)), dma((lines - 1,)),
                dma((2, slots)), dma((2, slots)),
                dma((2, lines - 1)), dma((2, lines - 1)),
                dma((2, lines)), dma((2, lines)),
            ],
            compiler_params=pltpu.CompilerParams(
                collective_id=0, has_side_effects=True, vmem_limit_bytes=60 * 1024 * 1024,
            ),
        )(edge_in, edge_grad, row_mask, layer_at)

    in_specs = (
        P(None, ("dp", "owner"), None),
        P(None, ("dp", "owner"), None),
        P(None, ("dp", "owner")),
        P(),
    )
    return jax.shard_map(local, mesh=mesh, in_specs=in_specs, out_specs=P("owner", None, None), check_vma=False)
```

time: 52.5 us -> 45 us (0.86)
  Pallas kernels: 50.2 us -> 42.7 us
    pallas_call x1, Pallas kernels: 50.2 us -> 42.7 us  [local(): pl.pallas_call(functools.partial(kernel, owners, chips, slots, rows, widt...]
where the time goes in v3:
time: 45 us; the launch traced here: 44.6 us
  Pallas kernels  42.7 us (95%)
  local copies, waits for them, and re-layouts  1.87 us (4%)
    pallas_call x1, Pallas kernels, local(): pl.pallas_call(functools.partial(kernel, owners, chips, slots, rows, widt...  42.7 us
    unnamed x1, local copies, waits for them, and re-layouts  1.87 us

profile of v3, /device:TPU:1, one launch (start us, length us, event | category | flops | bytes accessed | tf_op | source)
XLA Modules:
  0.0 44.6 jit_solution(9816591490952847792)
XLA Ops:
  0.0 42.7 %shard_map.46 = bf16[1,512,512]{2,1,0:T(8,128)(2,1)} custom-call(bf16[2,256,512]{2,1,0:T(8,128)(2,1)} %edge_in.1, bf16[2,256,512]{2,1,0:T(8,128)(2,1)} %edge_grad.1, s32[2,256]{1,0:T(2,128)} %mask.1, s32[2]{0:T(128)} %layer_at.1), custom_call_target="tpu_custom_call" | custom-call | tf_op jit(solution)/shard_map/pallas_call | solution.py:231
  42.8 1.9 %copy.6 = bf16[1,512,512]{2,1,0:T(8,128)(2,1)} copy(bf16[1,512,512]{2,1,0:T(8,128)(2,1)} %shard_map.46) | data formatting | bytes 1048576

commit v4 on v3

--- a/solution.py
+++ b/solution.py
@@ -100,7 +100,15 @@
         return total[:, s, at].astype(F32).reshape(TILE, TILE)
 
     order = list(range(1, lines)) + [0]
+    early, middle = order[:2], order[2:-1]
+    late = [(0, order[0])] + [(o, k) for k in middle for o in range(1, owners)]
+    late += [(0, k) for k in order[1:-1]] + [(o, 0) for o in range(1, owners)] + [(0, 0)]
     pair_copies = {}
+
+    def send_pair(o, k):
+        far = lax.rem(line + k, lines) * 2 + 1 - side
+        pair_copies[o, k] = copy(split.at[o, :, far], pair_got.at[o, k], pair_send.at[o, k], pair_recv.at[o, k], pair)
+
     for o in list(range(1, owners)) + [0]:
         q = lax.rem(me + o, owners)
         core_copies = []
@@ -114,25 +122,23 @@
             core_copies[s].wait_recv()
             split[o, s] = (split[o, s].astype(F32) + got[o, s].astype(F32)).astype(BF16)
         started += core_copies
-        for k in order:
-            far = lax.rem(line + k, lines) * 2 + 1 - side
-            pair_copies[o, k] = copy(split.at[o, :, far], pair_got.at[o, k], pair_send.at[o, k], pair_recv.at[o, k], pair)
-
-    owner_copies = {}
-    for o in range(1, owners):
-        for k in order:
-            near = lax.rem(line + k, lines) * 2 + side
-            pair_copies[o, k].wait_recv()
-            crossing[o - 1, k] = (split[o, :, near].astype(F32) + pair_got[o, k].astype(F32)).astype(BF16)
+        for k in early if o else ():
+            send_pair(o, k)
+    for o, k in late:
+        send_pair(o, k)
+
+    owner_copies, line_copies = {}, {}
+    for o, k in [(o, k) for o in range(1, owners) for k in early] + late:
+        near = lax.rem(line + k, lines) * 2 + side
+        pair_copies[o, k].wait_recv()
+        summed = split[o, :, near].astype(F32) + pair_got[o, k].astype(F32)
+        if o:
+            crossing[o - 1, k] = summed.astype(BF16)
             owner_copies[o, k] = copy(crossing.at[o - 1, k], owner_got.at[o - 1, k], owner_send.at[o - 1, k], owner_recv.at[o - 1, k], owner_at(o))
-    line_copies = {}
-    for k in order:
-        near = lax.rem(line + k, lines) * 2 + side
-        pair_copies[0, k].wait_recv()
-        summed = split[0, :, near].astype(F32) + pair_got[0, k].astype(F32)
-        for o in range(1, owners):
-            owner_copies[o, k].wait_recv()
-            summed += owner_got[o - 1, k].astype(F32)
+            continue
+        for p in range(1, owners):
+            owner_copies[p, k].wait_recv()
+            summed += owner_got[p - 1, k].astype(F32)
         if k:
             passing[k - 1] = summed.astype(BF16)
             line_copies[k] = copy(passing.at[k - 1], line_got.at[k - 1], line_send.at[k - 1], line_recv.at[k - 1], line_at(k))

time: 45 us -> 43.2 us (0.960)
  Pallas kernels: 42.7 us -> 41.2 us
    pallas_call x1, Pallas kernels: 42.7 us -> 41.2 us  [local(): pl.pallas_call(functools.partial(kernel, owners, chips, slots, rows, widt...]
where the time goes in v4:
time: 43.2 us; the launch traced here: 43.1 us
  Pallas kernels  41.2 us (95%)
  local copies, waits for them, and re-layouts  1.87 us (4%)
    pallas_call x1, Pallas kernels, local(): pl.pallas_call(functools.partial(kernel, owners, chips, slots, rows, widt...  41.2 us
    unnamed x1, local copies, waits for them, and re-layouts  1.87 us

profile of v4, /device:TPU:1, one launch (start us, length us, event | category | flops | bytes accessed | tf_op | source)
XLA Modules:
  0.0 43.1 jit_solution(13012836632368935139)
XLA Ops:
  0.0 41.2 %shard_map.46 = bf16[1,512,512]{2,1,0:T(8,128)(2,1)} custom-call(bf16[2,256,512]{2,1,0:T(8,128)(2,1)} %edge_in.1, bf16[2,256,512]{2,1,0:T(8,128)(2,1)} %edge_grad.1, s32[2,256]{1,0:T(2,128)} %mask.1, s32[2]{0:T(128)} %layer_at.1), custom_call_target="tpu_custom_call" | custom-call | tf_op jit(solution)/shard_map/pallas_call | solution.py:237
  41.2 1.9 %copy.6 = bf16[1,512,512]{2,1,0:T(8,128)(2,1)} copy(bf16[1,512,512]{2,1,0:T(8,128)(2,1)} %shard_map.46) | data formatting | bytes 1048576
